TPU v7x, 512 devices: a 8x2x16 block of a 8x8x16 slice. The times are simulated.
512 devices in a mesh: groups: 2 (over y), range: 128 (over z, x), sub: 2 (over core).
Axes of the slice: x: 8, y: 2, z: 16, core: 2. Of those that a mesh axis runs over, the one named last changes fastest.
The devices are a block of a 8x8x16 slice.
Arguments:
- samples: float32 [2, 1024, 512, 128], P(None, ('groups', 'range', 'sub')), parts along dimension 1, may hold values from -6 to 6
- beam_weights: float32 [512, 8, 2, 64, 128], P(('groups', 'range'), None, None, None, 'sub'), parts along dimension 0, may hold values from -0.25 to 0.25
- subarrays: int32 [512, 8, 64], P(('groups', 'range', 'sub')), parts along dimension 0, may hold values from 0 to 511, as said below
- training: int32 [1024], P(('groups', 'range', 'sub')), parts along dimension 0, may hold values 0 or 1
Outputs:
- covariance: float32 [512, 8, 64, 128], P(('groups', 'range', 'sub')), parts along dimension 0
- filtered: float32 [2, 128, 1024, 128], P(None, None, ('groups', 'range', 'sub')), parts along dimension 2
- energy: float32 [256], P('groups'), parts along dimension 0
There are 2 independent parts, one for each index of `groups`. A program takes and returns all parts, laid end to end along the dimension named above; each array names one. Nothing has to cross between parts.
Inputs may be any that keep to these rules, and one draw needn't show every extreme that they name: `subarrays`: in each gate block the 512 indices are all 512 channels, each once.
All inputs are finite; a program needn't handle non-finite values. No bound on the sum of `training` on one device may be relied on, other than what follows from the above.
Results may differ from a plain program's by a relative error of at most 0.0003.
Values sent between devices are 32-bit elements; how exact they have to be, the bound alone decides.
A program may use at most 64 MiB of HBM per device.

v0:
```python
import functools

import jax
import jax.numpy as jnp
from jax import lax
from jax.sharding import Mesh
from jax.sharding import PartitionSpec as P

GB = 2
RANGE = ("range_0", "range_1")
RANGE_SUB = ("range_0", "range_1", "sub")
GROUPS_RANGE_SUB = ("groups", "range_0", "range_1", "sub")
GROUPS_RANGE = ("groups", "range_0", "range_1")


loading = 0.05


def split_up(array, dim, peers):
    lengths = array.shape
    parts = array.reshape(*lengths[:dim], peers, lengths[dim] // peers, *lengths[dim + 1 :])
    return jnp.moveaxis(parts, dim, 0)


def joined_along(parts, dim):
    lengths = list(parts.shape[1:])
    lengths[dim] *= parts.shape[0]
    return jnp.moveaxis(parts, 0, dim).reshape(lengths)


def one_exchange(array, axis, axes, splits, concats):
    sizes = [lax.axis_size(a) for a in axes]
    parts = split_up(array, splits[0], sizes[0])
    parts = jnp.moveaxis(split_up(parts, splits[1] + 1, sizes[1]), 0, 1)
    inside = parts.shape[2:]
    parts = parts.reshape(-1, *inside)
    parts = lax.all_to_all(parts, axis, split_axis=0, concat_axis=0, tiled=True)
    parts = joined_along(parts.reshape(*sizes, *inside), concats[0] + 1)
    return joined_along(parts, concats[1])


def by_axis(array, axes):
    return functools.reduce(lax.psum, axes, array)


def block_terms(snaps, chosen, weights, masked, factor):
    highest = lax.Precision.HIGHEST
    picked = jnp.take(snaps, chosen, axis=1)
    real_part = picked[0]
    imag_part = picked[1]
    real_masked = real_part * masked
    imag_masked = imag_part * masked
    cov_real = (
        jnp.einsum("snx,smx->snm", real_masked, real_part, precision=highest)
        + jnp.einsum("snx,smx->snm", imag_masked, imag_part, precision=highest)
    ) * factor
    cov_imag = (
        jnp.einsum("snx,smx->snm", imag_masked, real_part, precision=highest)
        - jnp.einsum("snx,smx->snm", real_masked, imag_part, precision=highest)
    ) * factor
    w_real = weights[:, 0]
    w_imag = weights[:, 1]
    out_real = jnp.einsum("snk,snx->kx", w_real, real_part, precision=highest) + jnp.einsum(
        "snk,snx->kx", w_imag, imag_part, precision=highest
    )
    out_imag = jnp.einsum("snk,snx->kx", w_real, imag_part, precision=highest) - jnp.einsum(
        "snk,snx->kx", w_imag, real_part, precision=highest
    )
    prod_real = jnp.einsum("snm,smk->snk", cov_real, w_real, precision=highest) - jnp.einsum(
        "snm,smk->snk", cov_imag, w_imag, precision=highest
    )
    prod_imag = jnp.einsum("snm,smk->snk", cov_real, w_imag, precision=highest) + jnp.einsum(
        "snm,smk->snk", cov_imag, w_real, precision=highest
    )
    quadratic = jnp.sum(w_real * prod_real + w_imag * prod_imag, axis=(0, 1))
    inverse = 1.0 / jnp.sqrt(quadratic + loading)
    filtered = jnp.stack([out_real * inverse[:, None], out_imag * inverse[:, None]])
    energy = jnp.sum(out_real * out_real + out_imag * out_imag, axis=1)
    covariance = jnp.concatenate([cov_real, cov_imag], axis=-1)
    return (covariance, filtered, energy)


def body(samples, beam_weights, subarrays, training):
    range_count = lax.axis_size(RANGE)
    core_count = lax.axis_size("sub")
    parts_iq, chan_dev, all_gates, pulses = samples.shape
    gate_dev = all_gates // (range_count * core_count)
    channels = chan_dev * range_count * core_count
    blocks_dev = gate_dev // GB
    spread = samples.reshape(parts_iq, 1, 1, chan_dev, range_count, core_count, gate_dev, pulses)
    turned = one_exchange(spread, RANGE_SUB, (RANGE, "sub"), (4, 5), (1, 2))
    local_data = turned.reshape(parts_iq, channels, blocks_dev, GB * pulses).transpose(2, 0, 1, 3)
    mine = lax.all_to_all(beam_weights, "sub", split_axis=0, concat_axis=4, tiled=True)
    gates_on = training.astype(jnp.float32).reshape(blocks_dev, GB)
    masked = jnp.repeat(gates_on, pulses, axis=1)
    factor = 1.0 / (GB * pulses)
    covs, filts, energies = jax.vmap(block_terms, in_axes=(0, 0, 0, 0, None))(
        local_data, subarrays, mine, masked, factor
    )
    beams = filts.shape[2]
    filtered = filts.reshape(blocks_dev, parts_iq, beams, GB, pulses).transpose(1, 2, 0, 3, 4)
    filtered = filtered.reshape(parts_iq, beams, gate_dev, pulses)
    total = by_axis(jnp.sum(energies, axis=0), RANGE_SUB)
    energy = total / (all_gates * pulses)
    return (covs, filtered, energy)


def solution(mesh):
    torus = Mesh(
        mesh.devices.reshape(mesh.shape["groups"], 16, 8, mesh.shape["sub"]),
        ("groups", "range_0", "range_1", "sub"),
    )
    placed = (
        P(None, GROUPS_RANGE_SUB, None, None),
        P(GROUPS_RANGE, None, None, None, "sub"),
        P(GROUPS_RANGE_SUB, None, None),
        P(GROUPS_RANGE_SUB),
    )
    return jax.shard_map(
        body,
        mesh=torus,
        in_specs=placed,
        out_specs=(
            P(GROUPS_RANGE_SUB, None, None, None),
            P(None, None, GROUPS_RANGE_SUB, None),
            P("groups"),
        ),
        check_vma=False,
    )
```

profile of v0, /device:TPU:80, one launch (start us, length us, event | category | flops | bytes accessed | tf_op | source)
XLA Modules:
  0.0 180.7 jit_solution(4154683008116402408)
XLA Ops:
  0.6 0.0 copy-start
  0.6 2.5 %reshape.168 = f32[2,1,65536]{2,1,0:T(1,128)} reshape(f32[2,8,2,64,64]{4,3,2,1,0:T(8,128)} %param.5) | data formatting | bytes 1048576
  3.2 3.5 %all-to-all-start.1 = ((f32[2,1,65536]{2,1,0:T(1,128)}), f32[2,1,65536]{2,1,0:T(1,128)S(1)}, u32[]{:S(2)}, u32[]{:S(2)}) async-start(f32[2,1,65536]{2,1,0:T(1,128)} %reshape.168), calls=%async_computation.1 | async-start | bytes 1048576 | tf_op jit(solution)/shard_map/all_to_all | solution.py:93
  6.7 0.0 copy-done
  6.7 1.4 copy.16
  8.0 0.4 all-to-all-done.1
  8.4 0.0 copy-start.2
  8.4 0.0 copy-start.1
  8.4 61.1 %all-to-all-start = ((f32[256,2,1,1,2,1,1,2,128]{8,7,4,1,6,5,3,2,0:T(2,128)}), f32[256,2,1,1,2,1,1,2,128]{8,7,4,1,6,5,3,2,0:T(2,128)S(1)}, u32[]{:S(2)}, u32[]{:S(2)}) async-start(f32[256,2,1,1,2,1,1,2,128]{8,7,4,1,6,5,3,2,0:T(2,128)} %bitcast.5), calls=%async_computation | async-start | bytes 2097152 | tf_op jit(solution)/shard_map/all_to_all | solution.py:37
  69.5 0.0 copy-done.2
  69.5 0.0 copy-done.1
  69.5 0.1 reshape.158
  69.6 0.5 broadcast.75
  70.1 2.3 %reduce.5 = f32[2,65536]{1,0:T(2,128)S(1)} reduce(f32[2,1,65536]{2,1,0:T(1,128)S(1)} %all-to-all-done.1, f32[]{:T(128)} %broadcast.75), dimensions={1}, to_apply=%all_to_all.17.reduce_sub_computation | reduce | bytes 1048580 | tf_op jit(solution)/shard_map/all_to_all | solution.py:93
  72.4 0.6 reshape.169
  73.1 1.9 %copy.20 = f32[1,8,2,64,2,64]{5,4,3,1,2,0:T(2,128)} copy(f32[1,8,2,64,2,64]{5,3,2,1,4,0:T(8,128)S(1)} %bitcast.104) | data formatting | bytes 1048576 | tf_op jit(solution)/shard_map/all_to_all | solution.py:93
  74.9 1.8 %all_to_all.20 = f32[1,8,2,64,128]{4,3,1,2,0:T(8,128)S(1)} reshape(f32[1,8,2,64,2,64]{5,4,3,1,2,0:T(2,128)} %copy.20) | data formatting | bytes 1048576 | tf_op jit(solution)/shard_map/all_to_all | solution.py:93
  76.7 0.1 broadcast_bitcast_fusion
  76.8 43.3 %all-to-all-done = f32[256,2,1,1,2,1,1,2,128]{8,7,4,1,6,5,3,2,0:T(2,128)S(1)} async-done(((f32[256,2,1,1,2,1,1,2,128]{8,7,4,1,6,5,3,2,0:T(2,128)}), f32[256,2,1,1,2,1,1,2,128]{8,7,4,1,6,5,3,2,0:T(2,128)S(1)}, u32[]{:S(2)}, u32[]{:S(2)}) %all-to-all-start) | async-done | bytes 1048608 | tf_op jit(solution)/shard_map/all_to_all | solution.py:37
  120.1 0.4 copy.17
  120.5 0.8 copy.18
  121.3 2.6 %gather_fusion = f32[512,2,256]{2,1,0:T(2,128)S(1)} fusion(f32[1,2,512,256]{3,1,2,0:T(2,128)S(1)} %copy.18, s32[512]{0:T(512)S(1)} %reshape.158), kind=kCustom, calls=%fused_computation | custom fusion | bytes 2101248 | tf_op jit(solution)/shard_map/vmap(jit(_take))/gather | solution.py:48
  123.9 0.1 copy.19
  124.0 0.1 broadcast_select_fusion
  124.1 1.0 convolution_bitcast_fusion.2
  125.1 1.0 convolution_bitcast_fusion
  126.1 0.6 fusion.12
  126.8 0.6 fusion.2
  127.4 0.4 fusion.19
  127.8 0.4 fusion.18
  128.2 0.6 fusion.8
  128.8 1.0 fusion.6
  129.8 0.6 fusion.3
  130.4 0.4 fusion
  130.8 0.4 fusion.5
  131.3 1.0 add_reduce_fusion
  132.3 27.8 %psum.21 = f32[128]{0:T(128)S(1)} all-reduce(f32[128]{0:T(128)S(1)} %get-tuple-element.3), channel_id=1, replica_groups=mesh['groups'=2,'range_0'=16,'range_1'=8,'sub'=2] {'range_0'}, use_global_device_ids=true, to_apply=%region_2.3 | all-reduce | flops 128 | bytes 1024 | tf_op jit(solution)/shard_map/psum | solution.py:43
  160.1 15.7 %psum.22 = f32[128]{0:T(128)S(1)} all-reduce(f32[128]{0:T(128)S(1)} %psum.21), channel_id=1, replica_groups=mesh['groups'=2,'range_0'=16,'range_1'=8,'sub'=2] {'range_1'}, use_global_device_ids=true, to_apply=%region_3.4 | all-reduce | flops 128 | bytes 1024 | tf_op jit(solution)/shard_map/psum | solution.py:43
  175.8 2.5 %psum.23 = f32[128]{0:T(128)S(1)} all-reduce(f32[128]{0:T(128)S(1)} %psum.22), channel_id=1, replica_groups=mesh['groups'=2,'range_0'=16,'range_1'=8,'sub'=2] {'sub'}, use_global_device_ids=true, to_apply=%region_4.5 | all-reduce | flops 128 | bytes 1024 | tf_op jit(solution)/shard_map/psum | solution.py:43
  178.3 0.5 broadcast_multiply_fusion.2
  178.8 0.1 copy.21
  179.0 0.1 copy.22
  179.1 0.8 pad_maximum_fusion
  179.9 0.8 pad_maximum_fusion.1
  (6 shorter events, 0.0 us)
Async XLA Ops:
  0.6 6.0 %copy-start = (f32[2,2,512,128]{3,2,1,0:T(8,128)S(1)}, f32[2,2,512,128]{3,2,1,0:T(8,128)}, u32[]{:S(2)}) copy-start(f32[2,2,512,128]{3,2,1,0:T(8,128)} %param.4) | copy-start | bytes 3145732
  3.2 5.2 %all-to-all-start.1 = ((f32[2,1,65536]{2,1,0:T(1,128)}), f32[2,1,65536]{2,1,0:T(1,128)S(1)}, u32[]{:S(2)}, u32[]{:S(2)}) async-start(f32[2,1,65536]{2,1,0:T(1,128)} %reshape.168), calls=%async_computation.1 | async-start | bytes 1048576 | tf_op jit(solution)/shard_map/all_to_all | solution.py:93
  8.4 61.1 %copy-start.2 = (s32[2]{0:T(128)S(1)}, s32[2]{0:T(128)}, u32[]{:S(2)}) copy-start(s32[2]{0:T(128)} %param.7) | copy-start | bytes 28
  8.4 61.1 %copy-start.1 = (s32[1,8,64]{2,1,0:T(8,128)S(1)}, s32[1,8,64]{2,1,0:T(8,128)}, u32[]{:S(2)}) copy-start(s32[1,8,64]{2,1,0:T(8,128)} %param.6) | copy-start | bytes 6148
  8.4 111.7 %all-to-all-start = ((f32[256,2,1,1,2,1,1,2,128]{8,7,4,1,6,5,3,2,0:T(2,128)}), f32[256,2,1,1,2,1,1,2,128]{8,7,4,1,6,5,3,2,0:T(2,128)S(1)}, u32[]{:S(2)}, u32[]{:S(2)}) async-start(f32[256,2,1,1,2,1,1,2,128]{8,7,4,1,6,5,3,2,0:T(2,128)} %bitcast.5), calls=%async_computation | async-start | bytes 2097152 | tf_op jit(solution)/shard_map/all_to_all | solution.py:37
where the time goes:
time: 182 us; the launch traced here: 181 us
  starting transfers between devices  64.6 us (35%)
  blocking collectives  46 us (25%)
  waiting for transfers between devices  43.7 us (24%)
  local copies, waits for them, and re-layouts  12.9 us (7%)
  matrix products  8.13 us (4%)
  other arithmetic  4.67 us (3%)
    all_to_all x1, starting transfers between devices, one_exchange(): parts = lax.all_to_all(parts, axis, split_axis=0, concat_axis=0, tiled=True)  61.1 us
    psum x3, blocking collectives, by_axis(): return functools.reduce(lax.psum, axes, array)  46 us
    all_to_all x1, waiting for transfers between devices, one_exchange(): parts = lax.all_to_all(parts, axis, split_axis=0, concat_axis=0, tiled=True)  43.3 us
    all_to_all x3, local copies, waits for them, and re-layouts, body(): lax.all_to_all(beam_weights, 'sub', split_axis=0, concat_axis=4, tiled=True)  4.18 us
  transfers between devices with their start and end apart: 2, of which 2 were waited for; matrix products, arithmetic and copies ran while one was open for 4% of the time, Pallas kernels for 0%

commit v1 on v0

v1 whole, which is shorter than its diff:
```python
import functools

import jax
import jax.numpy as jnp
from jax import lax
from jax.experimental import pallas as pl
from jax.experimental.pallas import tpu as pltpu
from jax.sharding import PartitionSpec as P

F32 = jnp.float32
BF16 = jnp.bfloat16
GB = 2
NX = 8
GROUPS_RANGE_SUB = ("groups", "range", "sub")
GROUPS_RANGE = ("groups", "range")
loading = 0.05


def halves(value):
    high = value.astype(BF16)
    return high, (value - high.astype(F32)).astype(BF16)


def dot(left, right, across=False):
    dims = (((1,), (1 if across else 0,)), ((), ()))
    return lax.dot_general(left, right, dims, preferred_element_type=F32)


def dot3(left, right, across=False):
    (lh, ll), (rh, rl) = left, right
    return dot(lh, rh, across) + (dot(lh, rl, across) + dot(ll, rh, across))


def kernel(
    nz, nc, gates, x_ref, w_ref, sub_ref, train_ref,
    cov_ref, filt_ref, energy_ref,
    xv, zb, wb, sv, ev, ea, eb, mask, local_sem, send_sem, row_sem, arrived,
    w_send, w_recv, e_send, ea_sem, eb_sem,
):
    rng, core = lax.axis_index("range"), lax.axis_index("sub")
    z, x = rng // NX, rng % NX
    row = NX * nc
    rank = x * nc + core
    me = z * row + rank
    place = (z + nz - 1) % nz

    def at(z2, k):
        return {"range": z2 * NX + k // nc, "sub": k % nc}

    barrier = pltpu.get_barrier_semaphore()
    load = pltpu.make_async_copy(x_ref, xv, local_sem.at[0])
    load.start()

    def greet(i, _):
        pl.semaphore_signal(barrier, inc=1, device_id=at(z, (rank + 1 + i) % row))
        return 0

    lax.fori_loop(0, row - 1, greet, 0)

    @pl.when(place == 0)
    def _():
        pl.semaphore_wait(barrier, row - 1)

    @pl.when(place > 0)
    def _():
        pl.semaphore_wait(barrier, row)

    @pl.when(place < nz - 1)
    def _():
        pl.semaphore_signal(barrier, inc=1, device_id=at((z + 1) % nz, rank))

    def tell(i, _):
        pl.semaphore_signal(arrived.at[place], inc=1, device_id=at((z + nz - 1 - i) % nz, rank))
        return 0

    lax.fori_loop(0, place, tell, 0)
    load.wait()

    def send(z2, i, _):
        k = (rank + i) % row
        pltpu.make_async_remote_copy(
            src_ref=xv.at[:, pl.ds(gates * (z2 * row + k), gates), :],
            dst_ref=zb.at[:, pl.ds(gates * me, gates), :],
            send_sem=send_sem, recv_sem=row_sem.at[z], device_id=at(z2, k),
        ).start()
        return 0

    def send_row(z2):
        lax.fori_loop(0, row, functools.partial(send, z2), 0)

    def known(j, _):
        off = nz // 2 + lax.select(j % 2 == 0, j // 2, -(j // 2) - 1)

        @pl.when(off <= place)
        def _():
            send_row((z + nz - off) % nz)

        return 0

    lax.fori_loop(0, nz - 1, known, 0)
    lax.fori_loop(1, row, functools.partial(send, z), 0)

    def later(p, _):
        pl.semaphore_wait(arrived.at[p], 1)
        send_row((p + 1) % nz)
        return 0

    lax.fori_loop(place + 1, nz, later, 0)

    w_copy = pltpu.make_async_remote_copy(
        src_ref=w_ref.at[1 - core], dst_ref=wb.at[core], send_sem=w_send, recv_sem=w_recv,
        device_id={"sub": 1 - core},
    )
    w_copy.start()
    w_own = pltpu.make_async_copy(w_ref.at[core], wb.at[core], local_sem.at[1])
    w_own.start()
    s_own = pltpu.make_async_copy(sub_ref, sv, local_sem.at[2])
    s_own.start()
    t_own = pltpu.make_async_copy(train_ref, mask, local_sem.at[3])
    t_own.start()

    here = pl.ds(gates * me, gates)
    for plane in range(4):
        zb[plane, here, :] = xv[plane, here, :]

    s_own.wait()
    t_own.wait()
    w_own.wait()
    w_copy.wait()
    ns, _, width, half_beams = wb.shape[1:]
    beams = 2 * half_beams
    chans = ns * width
    flat = ns * 2 * width
    lane = lax.broadcasted_iota(jnp.int32, (beams, 2 * width), 1)
    first = lane < width
    wt = jnp.concatenate(
        [wb[h].reshape(flat, half_beams).T for h in range(2)], axis=0
    )
    wts = [wt[:, s * 2 * width : (s + 1) * 2 * width] for s in range(ns)]
    parts = [[], []]
    for s in range(0, ns, 2):
        a, b = wts[s], wts[s + 1]
        parts[0].append(jnp.where(first, a, pltpu.roll(b, width, 1)))
        parts[1].append(jnp.where(first, pltpu.roll(a, width, 1), b))
    wr, wi = (jnp.concatenate(p, axis=1) for p in parts)
    column = lax.broadcasted_iota(jnp.int32, (width, chans), 1)
    name = 2 * (column % (chans // 2)) + column // (chans // 2)
    eye = lax.broadcasted_iota(jnp.int32, (width, width), 0) == lax.broadcasted_iota(jnp.int32, (width, width), 1)
    rows = []
    for s in range(ns):
        line = jnp.broadcast_to(sv[s : s + 1, :].astype(F32), (width, width))
        chosen = jnp.sum(jnp.where(eye, line, 0.0), axis=1, keepdims=True)
        rows.append(jnp.where(chosen == name.astype(F32), 1.0, 0.0))
    pick = jnp.concatenate(rows, axis=0).astype(BF16)
    wr_h, wr_l = halves(wr)
    wi_h, wi_l = halves(wi)
    moved = dot(jnp.concatenate([wr_h, wr_l, wi_h, wi_l], axis=0), pick).astype(BF16)
    mr_h, mr_l, mi_h, mi_l = (moved[i * beams : (i + 1) * beams] for i in range(4))
    steer = tuple(
        jnp.concatenate([jnp.concatenate([r, i], axis=1), jnp.concatenate([-i, r], axis=1)], axis=0)
        for r, i in ((mr_h, mi_h), (mr_l, mi_l))
    )

    block = zb.at[:, pl.ds(0, gates * row), :]
    short = zb.at[:, pl.ds(0, gates * (row - 1)), :]

    def receive(z2, _):
        @pl.when(z2 == z)
        def _():
            pltpu.make_async_copy(short, short, row_sem.at[z2]).wait()

        @pl.when(z2 != z)
        def _():
            pltpu.make_async_copy(block, block, row_sem.at[z2]).wait()

        return 0

    lax.fori_loop(0, nz, receive, 0)

    peers = nz * row
    planes = [
        jnp.concatenate([zb[plane, pl.ds(g, peers, stride=gates), :] for g in range(gates)], axis=1)
        for plane in range(4)
    ]
    data = halves(jnp.concatenate(planes, axis=0))
    beam = dot3(steer, data)
    out_r, out_i = beam[:beams], beam[beams:]
    power = jnp.sum(out_r * out_r + out_i * out_i, axis=1, keepdims=True)
    eye_b = lax.broadcasted_iota(jnp.int32, (beams, beams), 0) == lax.broadcasted_iota(jnp.int32, (beams, beams), 1)
    ev[0] = jnp.sum(jnp.where(eye_b, power, 0.0), axis=0, keepdims=True)
    ea[rank] = ev[0]

    def share_row(i, _):
        pltpu.make_async_remote_copy(
            src_ref=ev.at[0], dst_ref=ea.at[rank], send_sem=e_send.at[0], recv_sem=ea_sem,
            device_id=at(z, (rank + i) % row),
        ).start()
        return 0

    lax.fori_loop(1, row, share_row, 0)

    got = [
        dot(pick, d[part * chans : (part + 1) * chans]).astype(BF16) for d in data for part in range(2)
    ]
    gate_of = lax.broadcasted_iota(jnp.int32, (2 * width, got[0].shape[1]), 1) // (got[0].shape[1] // gates)
    on = jnp.where(gate_of == 0, mask[0].astype(F32), mask[1].astype(F32)).astype(BF16)
    factor = 1.0 / got[0].shape[1]
    lane_s = lax.broadcasted_iota(jnp.int32, (width, 2 * width), 1) < width
    total = jnp.zeros((beams, 2 * width), F32)

    def subarray(s):
        cut = slice(s * width, (s + 1) * width)
        high = jnp.concatenate([got[0][cut], got[1][cut]], axis=0)
        low = jnp.concatenate([got[2][cut], got[3][cut]], axis=0)
        full = dot3((high * on, low * on), (high, low), across=True) * factor
        top, turned = full[:width], pltpu.roll(full[width:], width, 1)
        cov = turned + jnp.where(lane_s, top, -top)
        cov_ref[s] = cov
        matrix = jnp.concatenate([jnp.where(lane_s, cov, -cov), pltpu.roll(cov, width, 1)], axis=0)
        return dot3(halves(wts[s]), halves(matrix)) * wts[s]

    for s in range(ns):
        total = total + subarray(s)

    ra = ea.at[pl.ds(0, row - 1)]
    pltpu.make_async_copy(ra, ra, ea_sem).wait()
    ev[1] = jnp.sum(ea[...], axis=0)
    eb[z] = ev[1]

    def share_column(i, _):
        pltpu.make_async_remote_copy(
            src_ref=ev.at[1], dst_ref=eb.at[z], send_sem=e_send.at[1], recv_sem=eb_sem,
            device_id=at((z + i) % nz, rank),
        ).start()
        return 0

    lax.fori_loop(1, nz, share_column, 0)

    inverse = 1.0 / jnp.sqrt(jnp.sum(total, axis=1, keepdims=True) + loading)
    pulses = out_r.shape[1] // gates
    for part, out in enumerate((out_r, out_i)):
        scaled = out * inverse
        for g in range(gates):
            filt_ref[part, pl.ds(g, beams, stride=gates), :] = scaled[:, g * pulses : (g + 1) * pulses]

    every = zb.at[:, pl.ds(0, gates * (peers - 1)), :]
    pltpu.make_async_copy(every, every, send_sem).wait()
    pltpu.make_async_copy(ra, ra, e_send.at[0]).wait()
    rb = eb.at[pl.ds(0, nz - 1)]
    pltpu.make_async_copy(rb, rb, e_send.at[1]).wait()
    pltpu.make_async_copy(rb, rb, eb_sem).wait()
    energy_ref[...] = jnp.sum(eb[...], axis=0) * (1.0 / (peers * gates * pulses))


def body(samples, beam_weights, subarrays, training):
    range_count, nc = lax.axis_size("range"), lax.axis_size("sub")
    nz = range_count // NX
    parts_iq, chan_dev, all_gates, pulses = samples.shape
    gates = training.shape[0]
    _, ns, _, width, half_beams = beam_weights.shape
    beams = half_beams * nc
    anywhere = pl.BlockSpec(memory_space=pl.ANY)
    vmem = pl.BlockSpec(memory_space=pltpu.VMEM)
    dma, regular = pltpu.SemaphoreType.DMA, pltpu.SemaphoreType.REGULAR
    cov, filt, energy = pl.pallas_call(
        functools.partial(kernel, nz, nc, gates),
        out_shape=(
            jax.ShapeDtypeStruct((ns, width, 2 * width), F32),
            jax.ShapeDtypeStruct((parts_iq, beams * gates, pulses), F32),
            jax.ShapeDtypeStruct((1, beams), F32),
        ),
        in_specs=[anywhere] * 4,
        out_specs=(vmem, vmem, vmem),
        scratch_shapes=[
            pltpu.VMEM((parts_iq * chan_dev, all_gates, pulses), F32),
            pltpu.VMEM((parts_iq * chan_dev, all_gates, pulses), F32),
            pltpu.VMEM((nc, ns, 2, width, half_beams), F32),
            pltpu.VMEM((ns, width), jnp.int32),
            pltpu.VMEM((2, 1, beams), F32),
            pltpu.VMEM((NX * nc, 1, beams), F32),
            pltpu.VMEM((nz, 1, beams), F32),
            pltpu.SMEM((gates,), jnp.int32),
            dma((4,)),
            dma,
            dma((nz,)),
            regular((nz,)),
            dma,
            dma,
            dma((2,)),
            dma,
            dma,
        ],
        compiler_params=pltpu.CompilerParams(collective_id=1, has_side_effects=True),
    )(
        samples.reshape(parts_iq * chan_dev, all_gates, pulses),
        beam_weights,
        subarrays.reshape(ns, width),
        training,
    )
    return (
        cov.reshape(1, ns, width, 2 * width),
        filt.reshape(parts_iq, beams, gates, pulses),
        energy.reshape(beams),
    )


def solution(mesh):
    return jax.shard_map(
        body,
        mesh=mesh,
        in_specs=(
            P(None, GROUPS_RANGE_SUB, None, None),
            P(GROUPS_RANGE, None, None, None, "sub"),
            P(GROUPS_RANGE_SUB, None, None),
            P(GROUPS_RANGE_SUB),
        ),
        out_specs=(
            P(GROUPS_RANGE_SUB, None, None, None),
            P(None, None, GROUPS_RANGE_SUB, None),
            P("groups"),
        ),
        check_vma=False,
    )
```

time: 182 us -> 108 us (0.59)
  Pallas kernels: 0 us -> 104 us
  starting transfers between devices: 64.6 us -> 0 us
  blocking collectives: 46 us -> 0 us
  waiting for transfers between devices: 43.7 us -> 0 us
  local copies, waits for them, and re-layouts: 12.9 us -> 2.94 us
  matrix products: 8.13 us -> 0 us
  other arithmetic: 4.67 us -> 0 us
    pallas_call x0 -> x1, Pallas kernels: none -> 104 us  [body(): pl.pallas_call(functools.partial(kernel, nz, nc, gates), out_shape=(jax.S...]
    all_to_all x2 -> x0, starting transfers between devices: 64.6 us -> none  [the longest x1 61.1 us: one_exchange(): parts = lax.all_to_all(parts, axis, split_axis=0, concat_axis=0, tiled=True)]
    psum x3 -> x0, blocking collectives: 46 us -> none  [by_axis(): return functools.reduce(lax.psum, axes, array)]
    all_to_all x2 -> x0, waiting for transfers between devices: 43.7 us -> none  [the longest x1 43.3 us: one_exchange(): parts = lax.all_to_all(parts, axis, split_axis=0, concat_axis=0, tiled=True)]
    dot_general x12 -> x0, matrix products: 8.13 us -> none  [the longest x1 1.02 us: block_terms(): jnp.einsum('snk,snx->kx', w_real, imag_part, precision=highest)]
    all_to_all x3 -> x0, local copies, waits for them, and re-layouts: 4.18 us -> none  [body(): lax.all_to_all(beam_weights, 'sub', split_axis=0, concat_axis=4, tiled=True)]
    gather x4 -> x0, local copies, waits for them, and re-layouts: 2.72 us -> none  [block_terms(): picked = jnp.take(snaps, chosen, axis=1)]
    another operation x4 -> x0, local copies, waits for them, and re-layouts: 2.39 us -> none  [the longest x1 1.35 us: split_up(): array.reshape(*lengths[:dim], peers, lengths[dim] // peers, *lengths[dim...]
  transfers between devices with their start and end apart: 2 -> 0, of which waited for: 2 -> 0; matrix products, arithmetic and copies ran while one was open for 4% -> 0% of each run, Pallas kernels for 0% -> 0%
where the time goes in v1:
time: 108 us; the launch traced here: 107 us
  Pallas kernels  104 us (96%)
  local copies, waits for them, and re-layouts  2.94 us (3%)
    pallas_call x1, Pallas kernels, body(): pl.pallas_call(functools.partial(kernel, nz, nc, gates), out_shape=(jax.S...  104 us
    unnamed x7, local copies, waits for them, and re-layouts  2.94 us

profile of v1, /device:TPU:80, one launch (start us, length us, event | category | flops | bytes accessed | tf_op | source)
XLA Modules:
  0.0 107.4 jit_solution(16680887064415604592)
XLA Ops:
  0.6 103.8 %shard_map.67 = (f32[8,64,128]{2,1,0:T(8,128)}, f32[2,256,128]{2,1,0:T(8,128)}, f32[1,128]{1,0:T(1,128)}) custom-call(f32[4,512,128]{2,1,0:T(8,128)} %bitcast.5, f32[2,8,2,64,64]{4,3,2,1,0:T(8,128)} %w_ref.1, s32[8,64]{1,0:T(8,128)} %bitcast.8, s32[2]{0:T(128)} %train_ref.1), custom_call_target="tpu_custom_call" | custom-call | tf_op jit(solution)/shard_map/pallas_call | solution.py:265
  104.4 0.0 copy-start
  104.4 1.7 %copy.10 = f32[1,8,64,128]{3,2,1,0:T(8,128)} copy(f32[1,8,64,128]{3,2,1,0:T(8,128)} %bitcast.7) | data formatting | bytes 524288
  106.2 0.0 copy-done
  106.2 0.0 copy-start.1
  106.2 0.7 copy.11
  106.9 0.0 copy-done.1
  106.9 0.5 copy.12
Async XLA Ops:
  104.4 1.7 %copy-start = (f32[2,256,128]{2,1,0:T(8,128)S(1)}, f32[2,256,128]{2,1,0:T(8,128)}, u32[]{:S(2)}) copy-start(f32[2,256,128]{2,1,0:T(8,128)} %get-tuple-element.7) | copy-start | bytes 786436
  106.2 0.7 copy-start.1

commit v2 on v1

--- a/solution.py
+++ b/solution.py
@@ -9,7 +9,7 @@
 
 F32 = jnp.float32
 BF16 = jnp.bfloat16
-GB = 2
+GROUP = 4
 NX = 8
 GROUPS_RANGE_SUB = ("groups", "range", "sub")
 GROUPS_RANGE = ("groups", "range")
@@ -34,7 +34,7 @@
 def kernel(
     nz, nc, gates, x_ref, w_ref, sub_ref, train_ref,
     cov_ref, filt_ref, energy_ref,
-    xv, zb, wb, sv, ev, ea, eb, mask, local_sem, send_sem, row_sem, arrived,
+    xv, zb, wb, steer, data, sv, ev, ea, eb, mask, local_sem, send_sem, row_sem, arrived,
     w_send, w_recv, e_send, ea_sem, eb_sem,
 ):
     rng, core = lax.axis_index("range"), lax.axis_index("sub")
@@ -47,12 +47,15 @@
     def at(z2, k):
         return {"range": z2 * NX + k // nc, "sub": k % nc}
 
+    def outward(j, count):
+        return count // 2 + lax.select(j % 2 == 0, j // 2, -(j // 2) - 1)
+
     barrier = pltpu.get_barrier_semaphore()
     load = pltpu.make_async_copy(x_ref, xv, local_sem.at[0])
     load.start()
 
-    def greet(i, _):
-        pl.semaphore_signal(barrier, inc=1, device_id=at(z, (rank + 1 + i) % row))
+    def greet(j, _):
+        pl.semaphore_signal(barrier, inc=1, device_id=at(z, (rank + outward(j, row)) % row))
         return 0
 
     lax.fori_loop(0, row - 1, greet, 0)
@@ -89,7 +92,7 @@
         lax.fori_loop(0, row, functools.partial(send, z2), 0)
 
     def known(j, _):
-        off = nz // 2 + lax.select(j % 2 == 0, j // 2, -(j // 2) - 1)
+        off = outward(j, nz)
 
         @pl.when(off <= place)
         def _():
@@ -144,7 +147,8 @@
         parts[1].append(jnp.where(first, pltpu.roll(a, width, 1), b))
     wr, wi = (jnp.concatenate(p, axis=1) for p in parts)
     column = lax.broadcasted_iota(jnp.int32, (width, chans), 1)
-    name = 2 * (column % (chans // 2)) + column // (chans // 2)
+    span = gates * row * GROUP // 2
+    name = 2 * (column // (2 * span) * span + column % span) + column // span % 2
     eye = lax.broadcasted_iota(jnp.int32, (width, width), 0) == lax.broadcasted_iota(jnp.int32, (width, width), 1)
     rows = []
     for s in range(ns):
@@ -156,10 +160,12 @@
     wi_h, wi_l = halves(wi)
     moved = dot(jnp.concatenate([wr_h, wr_l, wi_h, wi_l], axis=0), pick).astype(BF16)
     mr_h, mr_l, mi_h, mi_l = (moved[i * beams : (i + 1) * beams] for i in range(4))
-    steer = tuple(
-        jnp.concatenate([jnp.concatenate([r, i], axis=1), jnp.concatenate([-i, r], axis=1)], axis=0)
-        for r, i in ((mr_h, mi_h), (mr_l, mi_l))
-    )
+    for q in range(nz // GROUP):
+        cut = slice(q * 2 * span, (q + 1) * 2 * span)
+        for half, (r, i) in enumerate(((mr_h[:, cut], mi_h[:, cut]), (mr_l[:, cut], mi_l[:, cut]))):
+            steer[half, q] = jnp.concatenate(
+                [jnp.concatenate([r, i], axis=1), jnp.concatenate([-i, r], axis=1)], axis=0
+            )
 
     block = zb.at[:, pl.ds(0, gates * row), :]
     short = zb.at[:, pl.ds(0, gates * (row - 1)), :]
@@ -175,15 +181,19 @@
 
         return 0
 
-    lax.fori_loop(0, nz, receive, 0)
-
     peers = nz * row
-    planes = [
-        jnp.concatenate([zb[plane, pl.ds(g, peers, stride=gates), :] for g in range(gates)], axis=1)
-        for plane in range(4)
-    ]
-    data = halves(jnp.concatenate(planes, axis=0))
-    beam = dot3(steer, data)
+    beam = None
+    for q in (*range(1, nz // GROUP), 0):
+        lax.fori_loop(q * GROUP, (q + 1) * GROUP, receive, 0)
+        planes = [
+            jnp.concatenate(
+                [zb[plane, pl.ds(gates * q * span + g, span, stride=gates), :] for g in range(gates)], axis=1
+            )
+            for plane in range(4)
+        ]
+        data[0, q], data[1, q] = halves(jnp.concatenate(planes, axis=0))
+        term = dot3((steer[0, q], steer[1, q]), (data[0, q], data[1, q]))
+        beam = term if beam is None else beam + term
     out_r, out_i = beam[:beams], beam[beams:]
     power = jnp.sum(out_r * out_r + out_i * out_i, axis=1, keepdims=True)
     eye_b = lax.broadcasted_iota(jnp.int32, (beams, beams), 0) == lax.broadcasted_iota(jnp.int32, (beams, beams), 1)
@@ -200,7 +210,14 @@
     lax.fori_loop(1, row, share_row, 0)
 
     got = [
-        dot(pick, d[part * chans : (part + 1) * chans]).astype(BF16) for d in data for part in range(2)
+        dot(
+            pick,
+            jnp.concatenate(
+                [data[half, q, pl.ds(part * 2 * span, 2 * span), :] for q in range(nz // GROUP)], axis=0
+            ),
+        ).astype(BF16)
+        for half in range(2)
+        for part in range(2)
     ]
     gate_of = lax.broadcasted_iota(jnp.int32, (2 * width, got[0].shape[1]), 1) // (got[0].shape[1] // gates)
     on = jnp.where(gate_of == 0, mask[0].astype(F32), mask[1].astype(F32)).astype(BF16)
@@ -250,6 +267,15 @@
     pltpu.make_async_copy(rb, rb, e_send.at[1]).wait()
     pltpu.make_async_copy(rb, rb, eb_sem).wait()
     energy_ref[...] = jnp.sum(eb[...], axis=0) * (1.0 / (peers * gates * pulses))
+
+
+def writer(*refs):
+    sem = refs[-1]
+    copies = [pltpu.make_async_copy(refs[i], refs[i + 3], sem.at[i]) for i in range(3)]
+    for copy in copies:
+        copy.start()
+    for copy in copies:
+        copy.wait()
 
 
 def body(samples, beam_weights, subarrays, training):
@@ -265,9 +291,9 @@
     cov, filt, energy = pl.pallas_call(
         functools.partial(kernel, nz, nc, gates),
         out_shape=(
-            jax.ShapeDtypeStruct((ns, width, 2 * width), F32),
-            jax.ShapeDtypeStruct((parts_iq, beams * gates, pulses), F32),
-            jax.ShapeDtypeStruct((1, beams), F32),
+            pltpu.VMEM((ns, width, 2 * width), F32),
+            pltpu.VMEM((parts_iq, beams * gates, pulses), F32),
+            pltpu.VMEM((1, beams), F32),
         ),
         in_specs=[anywhere] * 4,
         out_specs=(vmem, vmem, vmem),
@@ -275,6 +301,8 @@
             pltpu.VMEM((parts_iq * chan_dev, all_gates, pulses), F32),
             pltpu.VMEM((parts_iq * chan_dev, all_gates, pulses), F32),
             pltpu.VMEM((nc, ns, 2, width, half_beams), F32),
+            pltpu.VMEM((2, nz // GROUP, 2 * beams, 4 * NX * nc * GROUP), BF16),
+            pltpu.VMEM((2, nz // GROUP, 4 * NX * nc * GROUP, gates * pulses), BF16),
             pltpu.VMEM((ns, width), jnp.int32),
             pltpu.VMEM((2, 1, beams), F32),
             pltpu.VMEM((NX * nc, 1, beams), F32),
@@ -297,6 +325,14 @@
         subarrays.reshape(ns, width),
         training,
     )
+    results = tuple(pltpu.with_memory_space_constraint(r, pltpu.VMEM) for r in (cov, filt, energy))
+    cov, filt, energy = pl.pallas_call(
+        writer,
+        out_shape=tuple(jax.ShapeDtypeStruct(r.shape, F32) for r in results),
+        in_specs=[vmem] * 3,
+        out_specs=(anywhere,) * 3,
+        scratch_shapes=[dma((3,))],
+    )(*results)
     return (
         cov.reshape(1, ns, width, 2 * width),
         filt.reshape(parts_iq, beams, gates, pulses),

time: 108 us -> 104 us (0.963)
  local copies, waits for them, and re-layouts: 2.94 us -> 0 us
    unnamed x7 -> x0, local copies, waits for them, and re-layouts: 2.94 us -> none
    pallas_call x1 -> x2, Pallas kernels: 104 us -> 103 us  [the longest x1 102 us: body(): pl.pallas_call(functools.partial(kernel, nz, nc, gates), out_shape=(pltpu...]
where the time goes in v2:
time: 104 us
  Pallas kernels  103 us (99%)
    pallas_call x1, Pallas kernels, body(): pl.pallas_call(functools.partial(kernel, nz, nc, gates), out_shape=(pltpu...  102 us

profile of v2, /device:TPU:80, one launch (start us, length us, event | category | flops | bytes accessed | tf_op | source)
XLA Modules:
  0.0 103.9 jit_solution(17978679968797584100)
XLA Ops:
  0.6 102.5 %shard_map.67 = (f32[8,64,128]{2,1,0:T(8,128)S(1)}, f32[2,256,128]{2,1,0:T(8,128)S(1)}, f32[1,128]{1,0:T(1,128)S(1)}) custom-call(f32[4,512,128]{2,1,0:T(8,128)} %bitcast.5, f32[2,8,2,64,64]{4,3,2,1,0:T(8,128)} %w_ref.1, s32[8,64]{1,0:T(8,128)} %bitcast.6, s32[2]{0:T(128)} %train_ref.1), custom_call_target="tpu_custom_call" | custom-call | tf_op jit(solution)/shard_map/pallas_call | solution.py:291
  103.1 0.8 shard_map.68

commit v3 on v2

--- a/solution.py
+++ b/solution.py
@@ -89,7 +89,7 @@
         return 0
 
     def send_row(z2):
-        lax.fori_loop(0, row, functools.partial(send, z2), 0)
+        lax.fori_loop(0, row, functools.partial(send, z2), 0, unroll=row)
 
     def known(j, _):
         off = outward(j, nz)

time: 104 us -> 104 us (level)
  no operation moved by 1% of the time
where the time goes in v3:
time: 104 us
  Pallas kernels  103 us (99%)
    pallas_call x1, Pallas kernels, body(): pl.pallas_call(functools.partial(kernel, nz, nc, gates), out_shape=(pltpu...  102 us

profile of v3, /device:TPU:80, one launch (start us, length us, event | category | flops | bytes accessed | tf_op | source)
XLA Modules:
  0.0 103.8 jit_solution(9741915392067201504)
XLA Ops:
  0.6 102.3 %shard_map.67 = (f32[8,64,128]{2,1,0:T(8,128)S(1)}, f32[2,256,128]{2,1,0:T(8,128)S(1)}, f32[1,128]{1,0:T(1,128)S(1)}) custom-call(f32[4,512,128]{2,1,0:T(8,128)} %bitcast.5, f32[2,8,2,64,64]{4,3,2,1,0:T(8,128)} %w_ref.1, s32[8,64]{1,0:T(8,128)} %bitcast.6, s32[2]{0:T(128)} %train_ref.1), custom_call_target="tpu_custom_call" | custom-call | tf_op jit(solution)/shard_map/pallas_call | solution.py:291
  103.0 0.8 shard_map.68

commit v4 on v3

--- a/solution.py
+++ b/solution.py
@@ -58,7 +58,7 @@
         pl.semaphore_signal(barrier, inc=1, device_id=at(z, (rank + outward(j, row)) % row))
         return 0
 
-    lax.fori_loop(0, row - 1, greet, 0)
+    lax.fori_loop(0, row - 1, greet, 0, unroll=row - 1)
 
     @pl.when(place == 0)
     def _():
@@ -207,7 +207,7 @@
         ).start()
         return 0
 
-    lax.fori_loop(1, row, share_row, 0)
+    lax.fori_loop(1, row, share_row, 0, unroll=row - 1)
 
     got = [
         dot(
@@ -251,7 +251,7 @@
         ).start()
         return 0
 
-    lax.fori_loop(1, nz, share_column, 0)
+    lax.fori_loop(1, nz, share_column, 0, unroll=nz - 1)
 
     inverse = 1.0 / jnp.sqrt(jnp.sum(total, axis=1, keepdims=True) + loading)
     pulses = out_r.shape[1] // gates

time: 104 us -> 104 us (level)
  no operation moved by 1% of the time
where the time goes in v4:
time: 104 us
  Pallas kernels  103 us (99%)
    pallas_call x1, Pallas kernels, body(): pl.pallas_call(functools.partial(kernel, nz, nc, gates), out_shape=(pltpu...  102 us

profile of v4, /device:TPU:80, one launch (start us, length us, event | category | flops | bytes accessed | tf_op | source)
XLA Modules:
  0.0 103.8 jit_solution(2664229526077422330)
XLA Ops:
  0.6 102.3 %shard_map.67 = (f32[8,64,128]{2,1,0:T(8,128)S(1)}, f32[2,256,128]{2,1,0:T(8,128)S(1)}, f32[1,128]{1,0:T(1,128)S(1)}) custom-call(f32[4,512,128]{2,1,0:T(8,128)} %bitcast.5, f32[2,8,2,64,64]{4,3,2,1,0:T(8,128)} %w_ref.1, s32[8,64]{1,0:T(8,128)} %bitcast.6, s32[2]{0:T(128)} %train_ref.1), custom_call_target="tpu_custom_call" | custom-call | tf_op jit(solution)/shard_map/pallas_call | solution.py:291
  103.0 0.8 shard_map.68
